TPU v7x, 1024 devices: a whole 8x8x8 slice. The times are simulated.
1024 devices in a mesh: tp: 64 (over y, x), dp: 16 (over z, core).
Axes of the slice: x: 8, y: 8, z: 8, core: 2. Of those that a mesh axis runs over, the one named last changes fastest.
Arguments:
- grad_out: bfloat16 [2048, 16384], P('dp', 'tp'), may hold values from -6 to 6
- hidden_sum: bfloat16 [2048, 16384], P('dp', 'tp'), may hold values from -100 to 100
- norm_gain: float32 [16384], P('tp'), may hold values from 0.5 to 1.5
- out_weight: bfloat16 [16384, 16384], P(None, 'tp'), may hold values from -0.046875 to 0.046875
Outputs:
- resid_grad: bfloat16 [2048, 16384], P('dp', 'tp')
- attn_grad: bfloat16 [2048, 16384], P('dp', 'tp')
- gain_grad: float32 [16384], P('tp')
All inputs are finite; a program needn't handle non-finite values.
Results may differ from a plain program's by a relative error of at most 0.0049.
Values sent between devices are 32-bit elements; how exact they have to be, the bound alone decides.
A program may use at most 64 MiB of HBM per device.

v0:
```python
import jax
import jax.numpy as jnp
from jax import lax
from jax.sharding import Mesh
from jax.sharding import PartitionSpec as P

D = 16384
TP = ("tp_0", "tp_1")


epsilon = 1e-05


def sent_to_all(array, axis):
    devices = lax.axis_size(axis)
    return lax.all_to_all(
        jnp.broadcast_to(array[None], (devices, *array.shape)), axis, 0, 0, tiled=True
    )


def taken_together(array, axis):
    return sent_to_all(array, axis).sum(axis=0)


def packed_total(arrays, axis):
    ends = [0]
    for a in arrays:
        ends.append(ends[-1] + a.size)
    running = taken_together(jnp.concatenate([a.ravel() for a in arrays]), axis)
    return tuple((running[b:e].reshape(a.shape) for a, b, e in zip(arrays, ends, ends[1:])))


def summed_rows(array, axes, dim):
    if not axes:
        return array
    nearer = lax.psum_scatter(array, axes[0], scatter_dimension=dim, tiled=True)
    return summed_rows(nearer, axes[1:], dim)


def on_device(grad_out, hidden_sum, norm_gain, out_weight):
    upstream = grad_out.astype(jnp.float32)
    stream = hidden_sum.astype(jnp.float32)
    scaled = norm_gain * upstream
    squares, dotted = packed_total(
        (jnp.sum(stream * stream, axis=1), jnp.sum(scaled * stream, axis=1)), TP
    )
    inverse = lax.rsqrt(squares / D + epsilon)
    normed = stream * inverse[:, None]
    resid_full = inverse[:, None] * (scaled - normed * (inverse * dotted / D)[:, None])
    gain_grad = taken_together(jnp.sum(upstream * normed, axis=0), "dp")
    resid_grad = resid_full.astype(jnp.bfloat16)
    partial_value = lax.dot_general(
        resid_grad, out_weight, (((1,), (1,)), ((), ())), preferred_element_type=jnp.float32
    )
    attn_grad = summed_rows(partial_value, TP, 1).astype(jnp.bfloat16)
    return (resid_grad, attn_grad, gain_grad)


def solution(mesh):
    finer = Mesh(mesh.devices.reshape(8, 8, mesh.shape["dp"]), ("tp_0", "tp_1", "dp"))
    return jax.shard_map(
        on_device,
        mesh=finer,
        in_specs=(P("dp", TP), P("dp", TP), P(TP), P(None, TP)),
        out_specs=(P("dp", TP), P("dp", TP), P(TP)),
        check_vma=False,
    )
```

profile of v0, /device:TPU:14, one launch (start us, length us, event | category | flops | bytes accessed | tf_op | source)
XLA Modules:
  0.0 201.0 jit_solution(12199222192821336468)
XLA Ops:
  7.2 0.0 reduce-scatter.3.cloned.1.call-start
  7.2 1.0 fusion.5
  8.3 26.0 %all_to_all.12 = f32[64,1,256]{2,1,0:T(1,128)S(1)} all-to-all(f32[64,1,256]{2,1,0:T(1,128)S(1)} %broadcast_in_dim.4), channel_id=1, replica_groups=mesh['tp_0'=8,'tp_1'=8,'dp'=16] {'tp_0','tp_1'}, dimensions={0} | all-to-all | bytes 131072 | tf_op jit(solution)/shard_map/all_to_all | solution.py:16
  34.3 0.1 reduce_sum.47
  34.4 1.0 fusion.4
  35.4 0.0 copy-start
  35.4 9.5 %fusion.7 = f32[128,16384]{1,0:T(8,128)} fusion(bf16[128,256]{1,0:T(8,128)(2,1)S(1)} %get-tuple-element.6, bf16[16384,256]{1,0:T(8,128)(2,1)} %param.7), kind=kOutput, calls=%fused_computation.15 | convolution fusion | flops 1073741824 | bytes 16842752 | tf_op jit(solution)/shard_map/dot_general | solution.py:52
  44.9 0.0 copy-done
  44.9 0.0 reduce-scatter.3.cloned.1.call-update
  44.9 0.0 reduce-scatter.5.cloned.1.call-start
  45.0 100.6 %reduce-scatter.3.cloned.1.call-done = f32[128,2048]{1,0:T(8,128)} async-done(((f32[128,16384]{1,0:T(8,128)}), f32[128,2048]{1,0:T(8,128)}) %reduce-scatter.3.cloned.1.call-update) | async-done | bytes 1048592 | tf_op jit(solution)/shard_map/reduce_scatter | solution.py:36
  145.5 0.0 reduce-scatter.5.cloned.1.call-update
  145.6 15.6 %all_to_all.13 = f32[16,1,256]{2,1,0:T(1,128)S(1)} all-to-all(f32[16,1,256]{2,1,0:T(1,128)S(1)} %broadcast_in_dim.5), channel_id=1, replica_groups=mesh['tp_0'=8,'tp_1'=8,'dp'=16] {'dp'}, dimensions={0} | all-to-all | bytes 32768 | tf_op jit(solution)/shard_map/all_to_all | solution.py:16
  161.2 0.6 reduce_sum.49
  161.8 30.8 %reduce-scatter.5.cloned.1.call-done = f32[128,256]{1,0:T(8,128)} async-done(((f32[128,2048]{1,0:T(8,128)}), f32[128,256]{1,0:T(8,128)}) %reduce-scatter.5.cloned.1.call-update) | async-done | bytes 131088 | tf_op jit(solution)/shard_map/reduce_scatter | solution.py:36
  192.7 1.5 convert_element_type.15
  (4 shorter events, 0.1 us)
Async XLA Ops:
  7.2 138.4 %reduce-scatter.3.cloned.1.call-start = ((), (), s32[]{:S(2)}) async-start(), calls=%async_computation.4 | async-start | bytes 9437184 | tf_op jit(solution)/shard_map/reduce_scatter | solution.py:36
  35.4 9.5 %copy-start = (bf16[128,256]{1,0:T(8,128)(2,1)}, bf16[128,256]{1,0:T(8,128)(2,1)S(1)}, u32[]{:S(2)}) copy-start(bf16[128,256]{1,0:T(8,128)(2,1)S(1)} %get-tuple-element.6) | copy-start | bytes 196612
  44.9 147.7 %reduce-scatter.5.cloned.1.call-start = ((), (), s32[]{:S(2)}) async-start(), calls=%async_computation.5 | async-start | bytes 1179648 | tf_op jit(solution)/shard_map/reduce_scatter | solution.py:36
Sparse Core Ops, SparseCore 0:
  45.0 100.4 reduce-scatter.2
  148.9 43.6 reduce-scatter.4
where the time goes:
time: 202 us; the launch traced here: 201 us
  waiting for transfers between devices  131 us (65%)
  blocking collectives  41.7 us (21%)
  between operations  14.1 us (7%)
  matrix products  9.46 us (5%)
  other arithmetic  4.24 us (2%)
    reduce_scatter x2, waiting for transfers between devices, summed_rows(): nearer = lax.psum_scatter(array, axes[0], scatter_dimension=dim, tiled=True)  131 us
    all_to_all x2, blocking collectives, sent_to_all(): lax.all_to_all(jnp.broadcast_to(array[None], (devices, *array.shape)), ax...  41.7 us
    dot_general x1, matrix products, on_device(): lax.dot_general(resid_grad, out_weight, (((1,), (1,)), ((), ())), preferr...  9.46 us
  transfers between devices with their start and end apart: 2, of which 2 were waited for; matrix products, arithmetic and copies ran while one was open for 0% of the time, Pallas kernels for 0%

commit v1 on v0

v1 whole, which is shorter than its diff:
```python
import functools

import jax
import jax.numpy as jnp
from jax import lax
from jax.experimental import pallas as pl
from jax.experimental.pallas import tpu as pltpu
from jax.sharding import Mesh
from jax.sharding import PartitionSpec as P

EPSILON = 1e-05
MESH = pl.DeviceIdType.MESH
LOADS = 4


def kernel(
    n, width,
    grad_hbm, stream_hbm, gain_hbm, weight_hbm,
    resid_out, attn_out, gain_out,
    grad_v, stream_v, gain_v, weight_v,
    scaled_t, stream_t, resid_t, operand, inverse_v,
    stat, stat_in, part, ring, turn, tail, final_t, gains,
    load_sem, stat_send, stat_recv, ring_send, ring_recv, tail_send, tail_recv, gain_send, gain_recv,
):
    y, x = lax.axis_index("y"), lax.axis_index("x")
    z, core = lax.axis_index("z"), lax.axis_index("core")
    half = n // 2
    here = {"x": x, "y": y}
    first_axis, second_axis = ("x", "y"), ("y", "x")
    rows = part.shape[-2]
    tokens = part.shape[-1]
    halved = rows // 2

    small = [
        pltpu.make_async_copy(s, d, load_sem.at[i])
        for i, (s, d) in enumerate(((grad_hbm, grad_v), (stream_hbm, stream_v), (gain_hbm, gain_v)))
    ]
    for load in small:
        load.start()
    span = weight_v.shape[0] // LOADS
    big = [
        pltpu.make_async_copy(
            weight_hbm.at[pl.ds(i * span, span)], weight_v.at[pl.ds(i * span, span)], load_sem.at[3 + i]
        )
        for i in range(LOADS)
    ]
    for load in big:
        load.start()

    zs = lax.axis_size("z")
    flips, bit = [{"core": 1 - core}], 1
    while bit < zs:
        flips.append({"z": z + bit - 2 * bit * lax.rem(z // bit, 2)})
        bit *= 2
    barrier = pltpu.get_barrier_semaphore()
    peers = [{a: lax.rem(here[a] + j, n)} for a in ("x", "y") for j in range(1, n)] + flips
    for peer in peers:
        pl.semaphore_signal(barrier, inc=1, device_id=peer, device_id_type=MESH)

    for load in small:
        load.wait()
    grad = grad_v[...].astype(jnp.float32)
    stream = stream_v[...].astype(jnp.float32)
    scaled_t[...] = jnp.transpose(gain_v[...] * grad)
    stream_t[...] = jnp.transpose(stream)
    stat[...] = jnp.zeros_like(stat)
    stat[0, 0:1, :] = jnp.sum(stream_t[...] * stream_t[...], axis=0, keepdims=True)
    stat[0, 1:2, :] = jnp.sum(scaled_t[...] * stream_t[...], axis=0, keepdims=True)
    pl.semaphore_wait(barrier, len(peers))

    def stat_copy(a, j):
        axis = ("x", "y")[a]
        return pltpu.make_async_remote_copy(
            src_ref=stat.at[a], dst_ref=stat_in.at[a, j],
            send_sem=stat_send.at[a, j], recv_sem=stat_recv.at[a, j],
            device_id={axis: lax.rem(here[axis] + j, n)}, device_id_type=MESH,
        )

    far_first = sorted(range(1, n), key=lambda j: -min(j, n - j))
    for a in range(2):
        for j in far_first:
            stat_copy(a, j).start()
        for j in reversed(far_first):
            stat_copy(a, j).wait_recv()
        both = stat[a]
        for j in range(1, n):
            both = both + stat_in[a, j]
        if a == 0:
            stat[1] = both
    inverse = lax.rsqrt(both[0:1] / width + EPSILON)
    factor = inverse * inverse * both[1:2] / width
    inverse_v[...] = jnp.broadcast_to(inverse, inverse_v.shape)
    resid = inverse * (scaled_t[...] - stream_t[...] * factor)
    resid_t[...] = resid
    operand[...] = resid.astype(jnp.bfloat16)
    for load in big:
        load.wait()

    def offset(c):
        return lax.rem(lax.select(lax.rem(c, 2) == 1, (n - 1 - c) // 2, half + c // 2), n)

    def multiply(c):
        o = offset(c)
        for h in range(2):
            for j in range(n):
                if h == 0:
                    yy, xx = lax.rem(y + o, n), lax.rem(x + j, n)
                else:
                    yy, xx = lax.rem(y + j, n), lax.rem(x + o, n)
                part[h, c, j] = jnp.dot(
                    weight_v[(yy * n + xx) * 2 + h], operand[...], preferred_element_type=jnp.float32
                )

    def side(d):
        return pl.ds(d * halved, halved)

    def ring_copy(h, d, c, s):
        axis = first_axis[h]
        if s == 1:
            src, dst = part.at[h, c, half, side(d)], ring.at[h, d, c, 0, side(d)]
        else:
            src, dst = ring.at[h, d, c, s - 2], ring.at[h, d, c, s - 1]
        return pltpu.make_async_remote_copy(
            src_ref=src, dst_ref=dst,
            send_sem=ring_send.at[h, d, c, s - 1], recv_sem=ring_recv.at[h, d, c, s - 1],
            device_id={axis: lax.rem(here[axis] + (1 if d == 0 else n - 1), n)}, device_id_type=MESH,
        )

    def tail_copy(h, d, s, last=False):
        axis = second_axis[h]
        if isinstance(s, int) and s == 1:
            src, dst = turn.at[h, side(d)], tail.at[h, d, 0, side(d)]
        else:
            src, dst = tail.at[h, d, s - 2], tail.at[h, d, s - 1]
        return pltpu.make_async_remote_copy(
            src_ref=src, dst_ref=dst,
            send_sem=tail_send.at[h, d, s - 1], recv_sem=tail_recv.at[h, d, s - 1],
            device_id={axis: lax.rem(here[axis] + 1 + d * (n - 2), n)}, device_id_type=MESH,
        )

    def begin(c):
        multiply(c)
        for h in range(2):
            for d in range(2):
                ring_copy(h, d, c, 1).start()

    def add(slot, other, d, s):
        if s == 1:
            slot[side(d)] += other[side(d)]
            slot[side(1 - d)] = other[side(1 - d)]
        else:
            slot[...] += other[...]

    def pass_on(c, s):
        m = half + 1 - s
        for h in range(2):
            for d in range(2):
                ring_copy(h, d, c, s - 1).wait_recv()
                add(ring.at[h, d, c, s - 2], part.at[h, c, m if d == 0 else n - m], d, s - 1)
                ring_copy(h, d, c, s).start()

    def sends_done(c):
        for h in range(2):
            for d in range(2):
                for s in range(1, half + 1):
                    ring_copy(h, d, c, s).wait_send()

    def arrive(c):
        for h in range(2):
            for d in range(2):
                ring_copy(h, d, c, half).wait_recv()
            turn_value = ring[h, 0, c, half - 1] + ring[h, 1, c, half - 1] + part[h, c, 0]

            @pl.when(c == 0)
            def _():
                turn[h] = turn_value
                for d in range(2):
                    tail_copy(h, d, 1).start()

            d = 1 - lax.rem(c, 2)
            for s in range(2, half + 1):

                @pl.when((c > 0) & ((c + 1) // 2 + 1 == s) & (c < n - 1))
                def _():
                    tail_copy(h, d, s - 1).wait_recv()
                    slot = tail.at[h, d, s - 2]
                    if s == 2:
                        other = pl.ds((1 - d) * halved, halved)
                        part[h, c, 0] = turn_value
                        slot[side(d)] += part[h, c, 0, side(d)]
                        slot[other] = part[h, c, 0, other]
                    else:
                        slot[...] += turn_value
                    tail_copy(h, d, s).start()

            @pl.when(c == n - 1)
            def _():
                for d in range(2):
                    tail_copy(h, d, half).wait_recv()
                final_t[h] = turn_value + tail[h, 0, half - 1] + tail[h, 1, half - 1]

    def gain_copy(k):
        return pltpu.make_async_remote_copy(
            src_ref=gains.at[0, k], dst_ref=gains.at[1, k],
            send_sem=gain_send.at[k], recv_sem=gain_recv.at[k],
            device_id=flips[k], device_id_type=MESH,
        )

    def aside(t):
        lanes = tokens

        @pl.when(t == 2)
        def _():
            column = jnp.transpose(jnp.broadcast_to(inverse_v[0:1], (tokens, tokens)))
            gains[0, 0] = jnp.zeros_like(gains[0, 0])
            for i in range(grad_v.shape[1] // lanes):
                at = pl.ds(i * lanes, lanes)
                product = grad_v[:, at].astype(jnp.float32) * stream_v[:, at].astype(jnp.float32) * column
                gains[0, 0, 0:1, at] = jnp.sum(product, axis=0, keepdims=True)
            gain_copy(0).start()

        for k in range(1, len(flips) + 1):

            @pl.when(t == 2 + k)
            def _():
                gain_copy(k - 1).wait_recv()
                total = gains[0, k - 1] + gains[1, k - 1]
                if k < len(flips):
                    gains[0, k] = total
                    gain_copy(k).start()
                else:
                    gain_out[...] = total[0:1]

        @pl.when(t == 1)
        def _():
            resid_out[...] = jnp.transpose(resid_t[...]).astype(jnp.bfloat16)

    begin(0)
    begin(1)

    def slot(t, _):
        @pl.when(t + 2 < n)
        def _():
            begin(t + 2)

        for s in range(2, half + 1):
            c = t - (s - 2)

            @pl.when((c >= 0) & (c < n))
            def _():
                pass_on(c, s)

        c = t - (half - 1)

        @pl.when((c >= 0) & (c < n))
        def _():
            arrive(c)

        @pl.when((c >= 1) & (c < n))
        def _():
            sends_done(c - 1)

        aside(t)
        return 0

    slots = n + half - 1
    assert slots > 2 + len(flips)
    lax.fori_loop(0, slots, slot, 0)

    for h in range(2):
        attn_out[:, pl.ds(h * rows, rows)] = jnp.transpose(final_t[h]).astype(jnp.bfloat16)

    sends_done(n - 1)
    for h in range(2):
        for d in range(2):
            for s in range(1, half + 1):
                tail_copy(h, d, s).wait_send()
    for k in range(len(flips)):
        gain_copy(k).wait_send()
    for a in range(2):
        for j in range(1, n):
            stat_copy(a, j).wait_send()


def on_device(n, zs, width, grad_out, hidden_sum, norm_gain, out_weight):
    tokens, features = grad_out.shape
    rows = features // 2
    half = n // 2
    groups = out_weight.shape[0] // rows
    flips = 1 + (zs - 1).bit_length()
    f32, bf16 = jnp.float32, jnp.bfloat16
    block = (rows, tokens)
    resid, attn, gains = pl.pallas_call(
        functools.partial(kernel, n, width),
        out_shape=(
            jax.ShapeDtypeStruct((tokens, features), bf16),
            jax.ShapeDtypeStruct((tokens, features), bf16),
            jax.ShapeDtypeStruct((1, features), f32),
        ),
        in_specs=[pl.BlockSpec(memory_space=pl.ANY)] * 4,
        out_specs=(pl.BlockSpec(memory_space=pltpu.VMEM),) * 3,
        scratch_shapes=[
            pltpu.VMEM((tokens, features), bf16),
            pltpu.VMEM((tokens, features), bf16),
            pltpu.VMEM((1, features), f32),
            pltpu.VMEM((groups, rows, features), bf16),
            pltpu.VMEM((features, tokens), f32),
            pltpu.VMEM((features, tokens), f32),
            pltpu.VMEM((features, tokens), f32),
            pltpu.VMEM((features, tokens), bf16),
            pltpu.VMEM((8, tokens), f32),
            pltpu.VMEM((2, 8, tokens), f32),
            pltpu.VMEM((2, n, 8, tokens), f32),
            pltpu.VMEM((2, n, n) + block, f32),
            pltpu.VMEM((2, 2, n, half) + block, f32),
            pltpu.VMEM((2,) + block, f32),
            pltpu.VMEM((2, 2, half) + block, f32),
            pltpu.VMEM((2,) + block, f32),
            pltpu.VMEM((2, flips, 8, features), f32),
            pltpu.SemaphoreType.DMA((3 + LOADS,)),
            pltpu.SemaphoreType.DMA((2, n)),
            pltpu.SemaphoreType.DMA((2, n)),
            pltpu.SemaphoreType.DMA((2, 2, n, half)),
            pltpu.SemaphoreType.DMA((2, 2, n, half)),
            pltpu.SemaphoreType.DMA((2, 2, half)),
            pltpu.SemaphoreType.DMA((2, 2, half)),
            pltpu.SemaphoreType.DMA((flips,)),
            pltpu.SemaphoreType.DMA((flips,)),
        ],
        compiler_params=pltpu.CompilerParams(
            collective_id=0, has_side_effects=True, vmem_limit_bytes=48 * 1024 * 1024
        ),
        name="fused",
    )(grad_out, hidden_sum, norm_gain.reshape(1, features), out_weight.reshape(groups, rows, features))
    return resid, attn, gains.reshape(features)


def solution(mesh, n=8, zs=8):
    finer = Mesh(mesh.devices.reshape(n, n, zs, 2), ("y", "x", "z", "core"))
    tp, dp = ("y", "x"), ("z", "core")

    def whole(grad_out, hidden_sum, norm_gain, out_weight):
        return jax.shard_map(
            functools.partial(on_device, n, zs, grad_out.shape[1]),
            mesh=finer,
            in_specs=(P(dp, tp), P(dp, tp), P(tp), P(None, tp)),
            out_specs=(P(dp, tp), P(dp, tp), P(tp)),
            check_vma=False,
        )(grad_out, hidden_sum, norm_gain, out_weight)

    return whole
```

time: 202 us -> 85.5 us (0.42)
  waiting for transfers between devices: 131 us -> 0 us
  Pallas kernels: 0 us -> 80.2 us
  blocking collectives: 41.7 us -> 0 us
  between operations: 14.1 us -> 0.65 us
  matrix products: 9.46 us -> 0 us
  other arithmetic: 4.24 us -> 0 us
  local copies, waits for them, and re-layouts: 0.05 us -> 4.17 us
    reduce_scatter x2 -> x0, waiting for transfers between devices: 131 us -> none  [summed_rows(): nearer = lax.psum_scatter(array, axes[0], scatter_dimension=dim, tiled=True)]
    pallas_call x0 -> x1, Pallas kernels: none -> 80.2 us  [on_device(): pl.pallas_call(functools.partial(kernel, n, width), out_shape=(jax.ShapeD...]
    all_to_all x2 -> x0, blocking collectives: 41.7 us -> none  [sent_to_all(): lax.all_to_all(jnp.broadcast_to(array[None], (devices, *array.shape)), ax...]
    dot_general x1 -> x0, matrix products: 9.46 us -> none  [on_device(): lax.dot_general(resid_grad, out_weight, (((1,), (1,)), ((), ())), preferr...]
    unnamed x2 -> x9, local copies, waits for them, and re-layouts: 0.01 us -> 4.17 us
    reduce_sum x4 -> x0, other arithmetic: 2.68 us -> none  [the longest x1 1.01 us: on_device(): gain_grad = taken_together(jnp.sum(upstream * normed, axis=0), 'dp')]
  transfers between devices with their start and end apart: 2 -> 0, of which waited for: 2 -> 0; matrix products, arithmetic and copies ran while one was open for 0% -> 0% of each run, Pallas kernels for 0% -> 0%
where the time goes in v1:
time: 85.5 us; the launch traced here: 85 us
  Pallas kernels  80.2 us (94%)
  local copies, waits for them, and re-layouts  4.17 us (5%)
    pallas_call x1, Pallas kernels, on_device(): pl.pallas_call(functools.partial(kernel, n, width), out_shape=(jax.ShapeD...  80.2 us
    unnamed x9, local copies, waits for them, and re-layouts  4.17 us

profile of v1, /device:TPU:14, one launch (start us, length us, event | category | flops | bytes accessed | tf_op | source)
XLA Modules:
  0.0 85.0 jit_solution(14581211320933510325)
XLA Ops:
  0.6 0.0 copy-start
  0.6 0.8 copy-done
  1.5 0.0 copy-start.1
  1.5 0.8 copy-done.1
  2.3 0.0 copy-start.2
  2.3 0.7 copy-done.2
  3.0 80.2 %fused.1 = (bf16[128,256]{1,0:T(8,128)(2,1)S(1)}, bf16[128,256]{1,0:T(8,128)(2,1)S(1)}, f32[1,256]{1,0:T(1,128)S(1)}) custom-call(bf16[128,256]{1,0:T(8,128)(2,1)S(1)} %copy-done, bf16[128,256]{1,0:T(8,128)(2,1)S(1)} %copy-done.1, f32[1,256]{1,0:T(1,128)S(1)} %bitcast.3, bf16[128,128,256]{2,1,0:T(8,128)(2,1)} %bitcast.5), custom_call_target="tpu_custom_call" | custom-call | tf_op jit(solution)/shard_map/fused/pallas_call | solution.py:293
  83.2 0.6 copy.10
  83.8 0.6 copy.11
  84.5 0.6 copy.12
Async XLA Ops:
  0.6 0.8 copy-start
  1.5 0.8 copy-start.1
  2.3 0.7 copy-start.2

commit v2 on v1

v2 whole, which is shorter than its diff:
```python
import functools

import jax
import jax.numpy as jnp
from jax import lax
from jax.experimental import pallas as pl
from jax.experimental.pallas import tpu as pltpu
from jax.sharding import Mesh
from jax.sharding import PartitionSpec as P

EPSILON = 1e-05
MESH = pl.DeviceIdType.MESH
EARLY = 2


def kernel(
    n, width,
    grad_hbm, stream_hbm, gain_hbm, weight_hbm,
    out, gain_out,
    grad_v, stream_v, gain_v, weight_v,
    scaled_t, stream_t, resid_t, operand, early, token_v,
    stat, stat_in, early_part, early_ring, part, ring, turn, tail, final_t, gains,
    load_sem, stat_send, stat_recv, early_send, early_recv, ring_send, ring_recv, tail_send, tail_recv, gain_send, gain_recv, entered,
):
    y, x = lax.axis_index("y"), lax.axis_index("x")
    z, core = lax.axis_index("z"), lax.axis_index("core")
    half = n // 2
    here = {"x": x, "y": y}
    first_axis, second_axis = ("x", "y"), ("y", "x")
    rows = part.shape[-2]
    tokens = part.shape[-1]
    halved = rows // 2

    small = [
        pltpu.make_async_copy(s, d, load_sem.at[i])
        for i, (s, d) in enumerate(((grad_hbm, grad_v), (stream_hbm, stream_v), (gain_hbm, gain_v)))
    ]
    for load in small:
        load.start()
    def offset(c):
        c = jnp.int32(c)
        return lax.rem(lax.select(lax.rem(c, 2) == 1, (n - 1 - c) // 2, half + c // 2), n)

    def weight_load(h, c):
        i = lax.rem(here[second_axis[h]] + offset(c), n)
        return pltpu.make_async_copy(
            weight_hbm.at[i, :, 0] if h == 0 else weight_hbm.at[:, i, 1], weight_v.at[h, i], load_sem.at[3 + h * n + c]
        )

    for c in range(n):
        for h in range(2):
            weight_load(h, c).start()

    zs = lax.axis_size("z")
    flips, uppers, bit = [{"core": 1 - core}], [], 1
    while bit < zs:
        upper = lax.rem(z // bit, 2)
        flips.append({"z": z + bit - 2 * bit * upper})
        uppers.append(upper)
        bit *= 2
    barrier = pltpu.get_barrier_semaphore()
    peers = [{a: lax.rem(here[a] + j, n)} for a in ("x", "y") for j in range(1, n)] + flips[:1]
    for peer in peers:
        pl.semaphore_signal(barrier, inc=1, device_id=peer, device_id_type=MESH)
    for k, upper in enumerate(uppers):

        @pl.when(upper == 0)
        def _():
            pl.semaphore_signal(barrier, inc=1, device_id=flips[1 + k], device_id_type=MESH)

    for load in small:
        load.wait()
    grad = grad_v[...].astype(jnp.float32)
    stream = stream_v[...].astype(jnp.float32)
    scaled_t[...] = jnp.transpose(gain_v[...] * grad)
    stream_t[...] = jnp.transpose(stream)
    stat[0, 0:1, :] = jnp.sum(stream_t[...] * stream_t[...], axis=0, keepdims=True)
    stat[0, 1:2, :] = jnp.sum(scaled_t[...] * stream_t[...], axis=0, keepdims=True)
    scaled = scaled_t[...]
    high = scaled.astype(jnp.bfloat16)
    early[0] = high
    early[1] = (scaled - high.astype(jnp.float32)).astype(jnp.bfloat16)
    early[2] = stream_t[...].astype(jnp.bfloat16)
    pl.semaphore_wait(barrier, len(peers) + sum(uppers))

    def stat_copy(a, j):
        axis = ("x", "y")[a]
        return pltpu.make_async_remote_copy(
            src_ref=stat.at[a], dst_ref=stat_in.at[a, j],
            send_sem=stat_send.at[a, j], recv_sem=stat_recv.at[a, j],
            device_id={axis: lax.rem(here[axis] + j, n)}, device_id_type=MESH,
        )

    def spot(h, j):
        return lax.rem(here[first_axis[h]] + j, n)

    def slab(h, o):
        blocks = weight_v[h, lax.rem(here[second_axis[h]] + o, n)]
        return blocks.reshape(n * rows, blocks.shape[-1])

    def product(a, b):
        return jnp.dot(a, b, preferred_element_type=jnp.float32)

    def multiply(c):
        for h in range(2):
            part[h, c] = product(slab(h, offset(c)), operand[...]).reshape(n, rows, tokens)

    def multiply_early(c):
        for h in range(2):
            blocks = slab(h, offset(c))
            value = product(blocks, early[0]) + product(blocks, early[1])
            early_part[h, c, 0] = value.reshape(n, rows, tokens)
            early_part[h, c, 1] = product(blocks, early[2]).reshape(n, rows, tokens)

    def side(d):
        return pl.ds(d * halved, halved)

    def ring_copy(h, d, c, s):
        axis = first_axis[h]
        if s == 1:
            src, dst = part.at[h, c, spot(h, half), side(d)], ring.at[h, d, c, 0, side(d)]
        else:
            src, dst = ring.at[h, d, c, s - 2], ring.at[h, d, c, s - 1]
        return pltpu.make_async_remote_copy(
            src_ref=src, dst_ref=dst,
            send_sem=ring_send.at[h, d, c, s - 1], recv_sem=ring_recv.at[h, d, c, s - 1],
            device_id={axis: lax.rem(here[axis] + (1 if d == 0 else n - 1), n)}, device_id_type=MESH,
        )

    def tail_copy(h, d, s, last=False):
        axis = second_axis[h]
        if isinstance(s, int) and s == 1:
            src, dst = turn.at[h, side(d)], tail.at[h, d, 0, side(d)]
        else:
            src, dst = tail.at[h, d, s - 2], tail.at[h, d, s - 1]
        return pltpu.make_async_remote_copy(
            src_ref=src, dst_ref=dst,
            send_sem=tail_send.at[h, d, s - 1], recv_sem=tail_recv.at[h, d, s - 1],
            device_id={axis: lax.rem(here[axis] + 1 + d * (n - 2), n)}, device_id_type=MESH,
        )

    def begin(c):
        multiply(c)
        for h in range(2):
            for d in range(2):
                ring_copy(h, d, c, 1).start()

    def early_copy(h, d, c, g, s):
        axis = first_axis[h]
        if s == 1:
            src, dst = early_part.at[h, c, g, spot(h, half), side(d)], early_ring.at[h, d, c, g, 0, side(d)]
        else:
            src, dst = early_ring.at[h, d, c, g, 0], early_ring.at[h, d, c, g, 1]
        return pltpu.make_async_remote_copy(
            src_ref=src, dst_ref=dst,
            send_sem=early_send.at[h, d, c, g, s - 1], recv_sem=early_recv.at[h, d, c, g, s - 1],
            device_id={axis: lax.rem(here[axis] + (1 if d == 0 else n - 1), n)}, device_id_type=MESH,
        )

    def begin_early(c):
        multiply_early(c)
        for g in range(2):
            for h in range(2):
                for d in range(2):
                    early_copy(h, d, c, g, 1).start()

    def add(slot, other, d, s):
        if s == 1:
            slot[side(d)] += other[side(d)]
            slot[side(1 - d)] = other[side(1 - d)]
        else:
            slot[...] += other[...]

    def ahead(d, s):
        m = half + 1 - s
        return m if d == 0 else n - m

    def pass_on(c, s):
        for h in range(2):
            for d in range(2):
                ring_copy(h, d, c, s - 1).wait_recv()
                add(ring.at[h, d, c, s - 2], part.at[h, c, spot(h, ahead(d, s))], d, s - 1)
                ring_copy(h, d, c, s).start()

    def pass_early(c):
        for g in range(2):
            for h in range(2):
                for d in range(2):
                    early_copy(h, d, c, g, 1).wait_recv()
                    add(early_ring.at[h, d, c, g, 0], early_part.at[h, c, g, spot(h, ahead(d, 2))], d, 1)
                    early_copy(h, d, c, g, 2).start()

    def join_early(c):
        multiply(c)
        for h in range(2):
            for d in range(2):
                for g in range(2):
                    early_copy(h, d, c, g, 2).wait_recv()
                joined = early_ring[h, d, c, 0, 1] - early_ring[h, d, c, 1, 1] * token_v[1, 0:1]
                ring[h, d, c, 1] = token_v[0, 0:1] * joined + part[h, c, spot(h, ahead(d, 3))]
                ring_copy(h, d, c, 3).start()

    def sends_done(c, first=1):
        for h in range(2):
            for d in range(2):
                for s in range(first, half + 1):
                    ring_copy(h, d, c, s).wait_send()

    def gathered(h, e):
        for d in range(2):
            ring_copy(h, d, e, half).wait_recv()
        return ring[h, 0, e, half - 1] + ring[h, 1, e, half - 1] + part[h, e, spot(h, 0)]

    def turn_first():
        for h in range(2):
            turn[h] = gathered(h, 0)
            for d in range(2):
                tail_copy(h, d, 1).start()

    def arrive(c):
        for h in range(2):
            turn_value = gathered(h, c)
            d = 1 - lax.rem(c, 2)
            for s in range(2, half + 1):

                @pl.when(((c + 1) // 2 + 1 == s) & (c < n - 1))
                def _():
                    tail_copy(h, d, s - 1).wait_recv()
                    slot = tail.at[h, d, s - 2]
                    if s == 2:
                        other = pl.ds((1 - d) * halved, halved)
                        mine = part.at[h, c, spot(h, 0)]
                        mine[...] = turn_value
                        slot[side(d)] += mine[side(d)]
                        slot[other] = mine[other]
                    else:
                        slot[...] += turn_value
                    tail_copy(h, d, s).start()

            @pl.when(c == n - 1)
            def _():
                for d in range(2):
                    tail_copy(h, d, half).wait_recv()
                final_t[h] = turn_value + tail[h, 0, half - 1] + tail[h, 1, half - 1]

    def gain_copy(k):
        return pltpu.make_async_remote_copy(
            src_ref=gains.at[0, k], dst_ref=gains.at[1, k],
            send_sem=gain_send.at[k], recv_sem=gain_recv.at[k],
            device_id=flips[k], device_id_type=MESH,
        )

    def write_resid():
        out[0:tokens] = jnp.transpose(resid_t[...]).astype(out.dtype)

    def gain_first():
        column = jnp.transpose(jnp.broadcast_to(token_v[0, 0:1], (tokens, tokens)))
        gains[0, 0] = jnp.zeros_like(gains[0, 0])
        for i in range(grad_v.shape[1] // tokens):
            at = pl.ds(i * tokens, tokens)
            value = grad_v[:, at].astype(jnp.float32) * stream_v[:, at].astype(jnp.float32) * column
            gains[0, 0, 0:1, at] = jnp.sum(value, axis=0, keepdims=True)
        gain_copy(0).start()

    def gain_step(k):
        gain_copy(k - 1).wait_recv()
        gains[0, k] = gains[0, k - 1] + gains[1, k - 1]

        @pl.when(uppers[k - 1] == 0)
        def _():
            pl.semaphore_wait(entered.at[k - 1], 1)

        gain_copy(k).start()

    def send_stats(a):
        for j in sorted(range(1, n), key=lambda j: -min(j, n - j)):
            stat_copy(a, j).start()

    def take_stats(a):
        for j in sorted(range(1, n), key=lambda j: min(j, n - j)):
            stat_copy(a, j).wait_recv()
        both = stat[a]
        for j in range(1, n):
            both = both + stat_in[a, j]
        return both

    send_stats(0)
    for k, upper in enumerate(uppers):

        @pl.when(upper == 1)
        def _():
            pl.semaphore_signal(entered.at[k], inc=1, device_id=flips[1 + k], device_id_type=MESH)

    for c in range(EARLY):
        for h in range(2):
            weight_load(h, c).wait()
        begin_early(c)
    for c in range(EARLY, n):
        for h in range(2):
            weight_load(h, c).wait()
    stat[1] = take_stats(0)
    send_stats(1)
    middle = EARLY + (n - EARLY) // 2
    front, back = (EARLY, middle), (middle, n)

    def each(chunks, do):
        lax.fori_loop(chunks[0], chunks[1], lambda c, _: (do(c), 0)[1], 0)

    for c in range(EARLY):
        pass_early(c)
    both = take_stats(1)
    inverse = lax.rsqrt(both[0:1] / width + EPSILON)
    factor = inverse * inverse * both[1:2] / width
    token_v[0] = jnp.broadcast_to(inverse, token_v.shape[1:])
    token_v[1] = jnp.broadcast_to(factor, token_v.shape[1:])
    resid = inverse * (scaled_t[...] - stream_t[...] * factor)
    resid_t[...] = resid
    operand[...] = resid.astype(jnp.bfloat16)

    each(front, begin)
    gain_first()
    each((0, EARLY), join_early)
    gain_step(1)
    each(front, lambda c: pass_on(c, 2))
    each((0, EARLY), lambda c: pass_on(c, 4))
    gain_step(2)
    each(front, lambda c: pass_on(c, 3))
    turn_first()
    each(back, begin)
    each(front, lambda c: pass_on(c, 4))
    gain_step(3)
    write_resid()
    each((1, 3), arrive)
    each(back, lambda c: pass_on(c, 2))
    each((3, 5), arrive)
    each(back, lambda c: pass_on(c, 3))
    each((0, EARLY), lambda c: sends_done(c, 3))
    each(front, sends_done)
    each(back, lambda c: pass_on(c, 4))
    each((5, n), arrive)

    for h in range(2):
        out[pl.ds(tokens, tokens), pl.ds(h * rows, rows)] = jnp.transpose(final_t[h]).astype(out.dtype)
    last = len(flips) - 1
    gain_copy(last).wait_recv()
    gain_out[...] = (gains[0, last] + gains[1, last])[0:1]

    each(back, sends_done)
    for h in range(2):
        for d in range(2):
            for c in range(EARLY):
                for g in range(2):
                    for s in range(1, 3):
                        early_copy(h, d, c, g, s).wait_send()
    for h in range(2):
        for d in range(2):
            for s in range(1, half + 1):
                tail_copy(h, d, s).wait_send()
    for k in range(len(flips)):
        gain_copy(k).wait_send()
    for a in range(2):
        for j in range(1, n):
            stat_copy(a, j).wait_send()


def on_device(n, zs, width, grad_out, hidden_sum, norm_gain, out_weight):
    tokens, features = grad_out.shape
    rows = features // 2
    half = n // 2
    flips = 1 + (zs - 1).bit_length()
    f32, bf16 = jnp.float32, jnp.bfloat16
    block = (rows, tokens)
    out, gains = pl.pallas_call(
        functools.partial(kernel, n, width),
        out_shape=(
            jax.ShapeDtypeStruct((2 * tokens, features), bf16),
            jax.ShapeDtypeStruct((1, features), f32),
        ),
        in_specs=[pl.BlockSpec(memory_space=pltpu.HBM)] * 4,
        out_specs=(pl.BlockSpec(memory_space=pltpu.VMEM),) * 2,
        scratch_shapes=[
            pltpu.VMEM((tokens, features), bf16),
            pltpu.VMEM((tokens, features), bf16),
            pltpu.VMEM((1, features), f32),
            pltpu.VMEM((2, n, n, rows, features), bf16),
            pltpu.VMEM((features, tokens), f32),
            pltpu.VMEM((features, tokens), f32),
            pltpu.VMEM((features, tokens), f32),
            pltpu.VMEM((features, tokens), bf16),
            pltpu.VMEM((3, features, tokens), bf16),
            pltpu.VMEM((2, 8, tokens), f32),
            pltpu.VMEM((2, 2, tokens), f32),
            pltpu.VMEM((2, n, 2, tokens), f32),
            pltpu.VMEM((2, EARLY, 2, n) + block, f32),
            pltpu.VMEM((2, 2, EARLY, 2, 2) + block, f32),
            pltpu.VMEM((2, n, n) + block, f32),
            pltpu.VMEM((2, 2, n, half) + block, f32),
            pltpu.VMEM((2,) + block, f32),
            pltpu.VMEM((2, 2, half) + block, f32),
            pltpu.VMEM((2,) + block, f32),
            pltpu.VMEM((2, flips, 8, features), f32),
            pltpu.SemaphoreType.DMA((3 + 2 * n,)),
            pltpu.SemaphoreType.DMA((2, n)),
            pltpu.SemaphoreType.DMA((2, n)),
            pltpu.SemaphoreType.DMA((2, 2, EARLY, 2, 2)),
            pltpu.SemaphoreType.DMA((2, 2, EARLY, 2, 2)),
            pltpu.SemaphoreType.DMA((2, 2, n, half)),
            pltpu.SemaphoreType.DMA((2, 2, n, half)),
            pltpu.SemaphoreType.DMA((2, 2, half)),
            pltpu.SemaphoreType.DMA((2, 2, half)),
            pltpu.SemaphoreType.DMA((flips,)),
            pltpu.SemaphoreType.DMA((flips,)),
            pltpu.SemaphoreType.REGULAR((flips - 1,)),
        ],
        compiler_params=pltpu.CompilerParams(
            collective_id=0, has_side_effects=True, vmem_limit_bytes=60 * 1024 * 1024
        ),
        name="fused",
    )(grad_out, hidden_sum, norm_gain.reshape(1, features), out_weight.reshape(n, n, 2, rows, features))
    return out[:tokens], out[tokens:], gains.reshape(features)


def solution(mesh, n=8, zs=8):
    finer = Mesh(mesh.devices.reshape(n, n, zs, 2), ("y", "x", "z", "core"))
    tp, dp = ("y", "x"), ("z", "core")

    def whole(grad_out, hidden_sum, norm_gain, out_weight):
        return jax.shard_map(
            functools.partial(on_device, n, zs, grad_out.shape[1]),
            mesh=finer,
            in_specs=(P(dp, tp), P(dp, tp), P(tp), P(None, tp)),
            out_specs=(P(dp, tp), P(dp, tp), P(tp)),
            check_vma=False,
        )(grad_out, hidden_sum, norm_gain, out_weight)

    return whole
```

time: 85.5 us -> 76.3 us (0.89)
  Pallas kernels: 80.2 us -> 72 us
  local copies, waits for them, and re-layouts: 4.17 us -> 2.74 us
    pallas_call x1, Pallas kernels: 80.2 us -> 72 us  [on_device(): pl.pallas_call(functools.partial(kernel, n, width), out_shape=(jax.ShapeD...]
    unnamed x9 -> x1, local copies, waits for them, and re-layouts: 4.17 us -> 1.21 us
    slice x0 -> x1, local copies, waits for them, and re-layouts: none -> 1.53 us  [on_device(): return (out[:tokens], out[tokens:], gains.reshape(features))]
where the time goes in v2:
time: 76.3 us; the launch traced here: 75.4 us
  Pallas kernels  72 us (94%)
  local copies, waits for them, and re-layouts  2.74 us (4%)
    pallas_call x1, Pallas kernels, on_device(): pl.pallas_call(functools.partial(kernel, n, width), out_shape=(jax.ShapeD...  72 us
    slice x1, local copies, waits for them, and re-layouts, on_device(): return (out[:tokens], out[tokens:], gains.reshape(features))  1.53 us

profile of v2, /device:TPU:14, one launch (start us, length us, event | category | flops | bytes accessed | tf_op | source)
XLA Modules:
  0.0 75.4 jit_solution(10942021519262888837)
XLA Ops:
  0.6 72.0 %fused.1 = (bf16[256,256]{1,0:T(8,128)(2,1)}, f32[1,256]{1,0:T(1,128)}) custom-call(bf16[128,256]{1,0:T(8,128)(2,1)} %grad_hbm.1, bf16[128,256]{1,0:T(8,128)(2,1)} %stream_hbm.1, f32[1,256]{1,0:T(1,128)} %bitcast.4, bf16[8,8,2,128,256]{4,3,2,1,0:T(8,128)(2,1)} %bitcast.3), custom_call_target="tpu_custom_call" | custom-call | tf_op jit(solution)/shard_map/fused/pallas_call | solution.py:373
  72.6 1.5 %fusion = (bf16[128,256]{1,0:T(8,128)(2,1)}, bf16[128,256]{1,0:T(8,128)(2,1)}) fusion(bf16[256,256]{1,0:T(8,128)(2,1)} %get-tuple-element.5), kind=kLoop, calls=%fused_computation | loop fusion | bytes 262144 | tf_op jit(solution)/shard_map/slice | solution.py:420
  74.1 1.2 %copy.8 = f32[256]{0:T(256)} copy(f32[256]{0:T(256)} %bitcast.5) | data formatting | bytes 2048

commit v3 on v2

--- a/solution.py
+++ b/solution.py
@@ -200,10 +200,10 @@
                 ring[h, d, c, 1] = token_v[0, 0:1] * joined + part[h, c, spot(h, ahead(d, 3))]
                 ring_copy(h, d, c, 3).start()
 
-    def sends_done(c, first=1):
+    def sends_done(c, first=1, last=half):
         for h in range(2):
             for d in range(2):
-                for s in range(first, half + 1):
+                for s in range(first, last + 1):
                     ring_copy(h, d, c, s).wait_send()
 
     def gathered(h, e):
@@ -318,15 +318,15 @@
     operand[...] = resid.astype(jnp.bfloat16)
 
     each(front, begin)
+    each(back, begin)
+    each((0, EARLY), join_early)
     gain_first()
-    each((0, EARLY), join_early)
     gain_step(1)
     each(front, lambda c: pass_on(c, 2))
     each((0, EARLY), lambda c: pass_on(c, 4))
     gain_step(2)
     each(front, lambda c: pass_on(c, 3))
     turn_first()
-    each(back, begin)
     each(front, lambda c: pass_on(c, 4))
     gain_step(3)
     write_resid()
@@ -336,31 +336,36 @@
     each(back, lambda c: pass_on(c, 3))
     each((0, EARLY), lambda c: sends_done(c, 3))
     each(front, sends_done)
-    each(back, lambda c: pass_on(c, 4))
-    each((5, n), arrive)
-
-    for h in range(2):
-        out[pl.ds(tokens, tokens), pl.ds(h * rows, rows)] = jnp.transpose(final_t[h]).astype(out.dtype)
-    last = len(flips) - 1
-    gain_copy(last).wait_recv()
-    gain_out[...] = (gains[0, last] + gains[1, last])[0:1]
-
-    each(back, sends_done)
     for h in range(2):
         for d in range(2):
             for c in range(EARLY):
                 for g in range(2):
                     for s in range(1, 3):
                         early_copy(h, d, c, g, s).wait_send()
-    for h in range(2):
-        for d in range(2):
-            for s in range(1, half + 1):
-                tail_copy(h, d, s).wait_send()
-    for k in range(len(flips)):
-        gain_copy(k).wait_send()
     for a in range(2):
         for j in range(1, n):
             stat_copy(a, j).wait_send()
+    for k in range(len(flips) - 1):
+        gain_copy(k).wait_send()
+    each(back, lambda c: pass_on(c, 4))
+    each(back, lambda c: sends_done(c, 1, half - 1))
+    for h in range(2):
+        for d in range(2):
+            for s in range(1, half):
+                tail_copy(h, d, s).wait_send()
+    each((5, n), arrive)
+
+    for h in range(2):
+        out[pl.ds(tokens, tokens), pl.ds(h * rows, rows)] = jnp.transpose(final_t[h]).astype(out.dtype)
+    last = len(flips) - 1
+    gain_copy(last).wait_recv()
+    gain_out[...] = (gains[0, last] + gains[1, last])[0:1]
+
+    each(back, lambda c: sends_done(c, half))
+    for h in range(2):
+        for d in range(2):
+            tail_copy(h, d, half).wait_send()
+    gain_copy(last).wait_send()
 
 
 def on_device(n, zs, width, grad_out, hidden_sum, norm_gain, out_weight):
@@ -373,8 +378,8 @@
     out, gains = pl.pallas_call(
         functools.partial(kernel, n, width),
         out_shape=(
-            jax.ShapeDtypeStruct((2 * tokens, features), bf16),
-            jax.ShapeDtypeStruct((1, features), f32),
+            pltpu.VMEM((2 * tokens, features), bf16),
+            pltpu.VMEM((1, features), f32),
         ),
         in_specs=[pl.BlockSpec(memory_space=pltpu.HBM)] * 4,
         out_specs=(pl.BlockSpec(memory_space=pltpu.VMEM),) * 2,

time: 76.3 us -> 73.6 us (0.965)
  local copies, waits for them, and re-layouts: 2.74 us -> 1.22 us
  Pallas kernels: 72 us -> 70.6 us
    pallas_call x1, Pallas kernels: 72 us -> 70.6 us  [on_device(): pl.pallas_call(functools.partial(kernel, n, width), out_shape=(pltpu.VMEM...]
    slice x1, local copies, waits for them, and re-layouts: 1.53 us -> 0.66 us  [on_device(): return (out[:tokens], out[tokens:], gains.reshape(features))]
where the time goes in v3:
time: 73.6 us; the launch traced here: 72.5 us
  Pallas kernels  70.6 us (96%)
  local copies, waits for them, and re-layouts  1.22 us (2%)
    pallas_call x1, Pallas kernels, on_device(): pl.pallas_call(functools.partial(kernel, n, width), out_shape=(pltpu.VMEM...  70.6 us

profile of v3, /device:TPU:14, one launch (start us, length us, event | category | flops | bytes accessed | tf_op | source)
XLA Modules:
  0.0 72.5 jit_solution(5334753352239762880)
XLA Ops:
  0.6 70.6 %fused.1 = (bf16[256,256]{1,0:T(8,128)(2,1)S(1)}, f32[1,256]{1,0:T(1,128)S(1)}) custom-call(bf16[128,256]{1,0:T(8,128)(2,1)} %grad_hbm.1, bf16[128,256]{1,0:T(8,128)(2,1)} %stream_hbm.1, f32[1,256]{1,0:T(1,128)} %bitcast.5, bf16[8,8,2,128,256]{4,3,2,1,0:T(8,128)(2,1)} %bitcast.4), custom_call_target="tpu_custom_call" | custom-call | tf_op jit(solution)/shard_map/fused/pallas_call | solution.py:378
  71.2 0.6 copy.8
  71.8 0.7 fusion
